TPU v7x, 128 devices: a whole 4x4x4 slice. The times are simulated.
128 devices in a mesh: batch: 1, graph: 128 (over z, y, x, core).
Axes of the slice: x: 4, y: 4, z: 4, core: 2. Of those that a mesh axis runs over, the one named last changes fastest.
Arguments:
- grid_in: float32 [65536, 186], P(('batch', 'graph'))
- mesh_in: float32 [32768, 3], P(('batch', 'graph'))
- edge_in: float32 [1048576, 4], P(('batch', 'graph'))
- edge_src: int32 [1048576], P(('batch', 'graph'))
- edge_dst: int32 [1048576], P(('batch', 'graph'))
- edge_mask: int32 [1048576], P(('batch', 'graph'))
- grid_w1: bfloat16 [186, 512], replicated
- grid_w2: bfloat16 [512, 512], replicated
- grid_vec: float32 [4, 512], replicated
- mesh_w1: bfloat16 [3, 512], replicated
- mesh_w2: bfloat16 [512, 512], replicated
- mesh_vec: float32 [4, 512], replicated
- embed_w1: bfloat16 [4, 512], replicated
- embed_w2: bfloat16 [512, 512], replicated
- embed_vec: float32 [4, 512], replicated
- edge_w1: bfloat16 [1536, 512], replicated
- edge_w2: bfloat16 [512, 512], replicated
- edge_vec: float32 [4, 512], replicated
- node_w1: bfloat16 [1024, 512], replicated
- node_w2: bfloat16 [512, 512], replicated
- node_vec: float32 [4, 512], replicated
- post_w1: bfloat16 [512, 512], replicated
- post_w2: bfloat16 [512, 512], replicated
- post_vec: float32 [4, 512], replicated
- cot_mesh: bfloat16 [32768, 512], P(('batch', 'graph'))
- cot_grid: bfloat16 [65536, 512], P(('batch', 'graph'))
Outputs:
- output 1: bfloat16 [32768, 512], P(('batch', 'graph'))
- output 2: bfloat16 [65536, 512], P(('batch', 'graph'))
- output 3: float32 [65536, 186], P(('batch', 'graph'))
- output 4: float32 [1536, 512], P(('batch', 'graph'))
- output 5: float32 [512, 512], P(('batch', 'graph'))
All inputs are finite; a program needn't handle non-finite values.
Results may differ from a plain program's by a relative error of at most 0.00869367.
Values are sent between devices in bfloat16 or wider.
A program may use at most 1 GiB of HBM per device.

v0:
```python
import jax
import jax.numpy as jnp
from jax import lax
from jax.experimental import pallas as pl
from jax.experimental.pallas import tpu as pltpu
from jax.sharding import PartitionSpec as P

NORM_EPS = 1e-5
BF = jnp.bfloat16
F32 = jnp.float32
VMEM = pltpu.VMEM
CHUNK = 512
FETCHED = (10, 13, 15, 18, 19, 21, 22, 25)
DEV = pl.DeviceIdType.MESH
GRID, MESH, EMBED, EDGE, NODE, POST = range(6)


def dot_nn(a, b):
    return jnp.dot(a, b, preferred_element_type=F32)


def dot_nt(a, b):
    return lax.dot_general(a, b, (((1,), (1,)), ((), ())), preferred_element_type=F32)


def dot_tn(a, b):
    return lax.dot_general(a, b, (((0,), (0,)), ((), ())), preferred_element_type=F32)


def split3(x):
    hi = x.astype(BF)
    rest = x - hi.astype(F32)
    mid = rest.astype(BF)
    low = (rest - mid.astype(F32)).astype(BF)
    return [hi, mid, low]


def silu_bf(p):
    h = 0.5 * p
    return (h + h * jnp.tanh(h)).astype(BF)


def norm_cols(q):
    centred = q - jnp.mean(q, axis=0, keepdims=True)
    inv = lax.rsqrt(jnp.mean(centred * centred, axis=0, keepdims=True) + NORM_EPS)
    return centred * inv, inv


def norm_back(d, n, inv):
    return inv * (d - jnp.mean(d, axis=0, keepdims=True) - n * jnp.mean(d * n, axis=0, keepdims=True))


def grad_first(d_act, p):
    t = jnp.tanh(0.5 * p)
    s = 0.5 + 0.5 * t
    return (d_act * (s * (1.0 + p * (1.0 - s)))).astype(BF)


def one_hot(rows, idx):
    return (lax.broadcasted_iota(jnp.int32, (rows, idx.shape[1]), 0) == idx).astype(F32).astype(BF)


def pick_lanes(ref, idx):
    outs = []
    for t in range(idx.shape[1] // 128):
        ix = idx[:, t * 128:(t + 1) * 128]
        low = jnp.broadcast_to(ix % 128, (ref.shape[0], 128))
        out = None
        for k in range(ref.shape[1] // 128):
            g = jnp.take_along_axis(ref[:, k * 128:(k + 1) * 128], low, axis=1, mode='promise_in_bounds')
            out = g if out is None else jnp.where(ix // 128 >= k, g, out)
        outs.append(out)
    return jnp.concatenate(outs, axis=1)


def lanes(*parts):
    return jnp.concatenate(parts, axis=1)


def rows(*parts):
    return jnp.concatenate(parts, axis=0)


def step_kernel(gx_ref, mx_ref, ex_ref, src_ref, dst_ref, mask_ref,
                gw1_ref, gw2_ref, gvec_ref, mw1_ref, mw2_ref, mvec_ref, ew1_ref, ew2_ref, evec_ref,
                dw1_ref, dw2_ref, dvec_ref, nw1_ref, nw2_ref, nvec_ref, pw1_ref, pw2_ref, pvec_ref,
                cotm_ref, cotg_ref,
                mesh_out_ref, grid_out_ref, ggrad_ref, o1_ref, o2_ref,
                pre_s, norm_s, he_s, inv_s, wl_s, pm_s, agg_s, g1_s, g2_s, act_s, cotg_s, w1g_s, w2g_s, table_s, hm_s, ew2t_s, dw2t_s, vt_s, vb_s, ew1t_s,
                stage_sem, done_sem, hs_sem, hr_sem, ts_sem, tr_sem, send0, recv0, sends, recvs, send4, recv4):
    lat = dw2_ref.shape[0]
    band = gx_ref.shape[1]
    nm = mx_ref.shape[1]
    halo = band // 4
    nt = band + 2 * halo
    ch = he_s.shape[1]
    steps = he_s.shape[0] // lat

    me = lax.axis_index('graph')
    total = 128
    core = lax.rem(me, 2)
    chip = me // 2
    px, py, pz = lax.rem(chip, 4), lax.rem(chip // 4, 4), chip // 16

    def dev(z, y, x, k):
        return {'graph': ((z * 4 + y) * 4 + x) * 2 + k}

    def turn(v, d):
        return lax.rem(v + d, 4)

    below = {'graph': lax.rem(me + total - 1, total)}
    above = {'graph': lax.rem(me + 1, total)}
    partner = dev(pz, py, px, 1 - core)
    peers = {'x': [dev(pz, py, turn(px, d), core) for d in (1, 2, 3)],
             'y': [dev(pz, turn(py, d), px, core) for d in (1, 2, 3)],
             'z': [dev(turn(pz, d), py, px, core) for d in (1, 2, 3)]}
    pos = {'x': px, 'y': py, 'z': pz}
    everyone = [below, above, partner] + peers['x'] + peers['y'] + peers['z']

    def fetch(k, src, slot):
        n = src.shape[0]
        return fetch_to(k, src, he_s.at[slot * lat:slot * lat + n, :])

    def fetch_to(k, src, dst):
        c = pltpu.make_async_copy(src, dst, stage_sem.at[k])
        c.start()
        return c

    def held(slot, n=1):
        return he_s[slot * lat:(slot + n) * lat, :]

    early = [fetch(0, mw2_ref, 15), fetch(1, dw1_ref, 10), fetch(2, ew2_ref, 14), fetch(4, pw1_ref, 5), fetch(5, pw2_ref, 6),
             fetch(6, cotg_ref, 7)]
    node = [fetch_to(7, nw1_ref.at[0:lat, :], g1_s), fetch_to(8, nw1_ref.at[lat:2 * lat, :], g2_s),
            fetch_to(9, nw2_ref, act_s)]

    barrier = pltpu.get_barrier_semaphore()
    for peer in everyone:
        pl.semaphore_signal(barrier, inc=1, device_id=peer, device_id_type=DEV)

    def copy(src, dst, ssem, rsem, peer):
        c = pltpu.make_async_remote_copy(src_ref=src, dst_ref=dst, send_sem=ssem, recv_sem=rsem, device_id=peer,
                                         device_id_type=DEV)
        c.start()
        return c

    v_s = pre_s.at[lat * steps - 128:lat * steps, :]
    v_s[...] = jnp.zeros(v_s.shape, F32)
    v_s[24:28, :] = ew1_ref[...].astype(F32)
    for k, ref in enumerate((gvec_ref, mvec_ref, evec_ref, dvec_ref, nvec_ref, pvec_ref)):
        v_s[4 * k:4 * k + 4, :] = ref[...]
    vt_s[...] = v_s[...].T
    ew1t_s[...] = vt_s[:, 24:28].astype(BF)

    def col(mlp, k):
        return vt_s[:, 4 * mlp + k:4 * mlp + k + 1]

    wide = [(EMBED, 0), (EMBED, 1), (EMBED, 2), (EMBED, 3), (EDGE, 1), (EDGE, 2), (EDGE, 3)]
    for j, (mlp, k) in enumerate(wide):
        vb_s[:, 128 * j:128 * (j + 1)] = jnp.broadcast_to(col(mlp, k), (lat, 128))

    def wcol(mlp, k):
        j = wide.index((mlp, k))
        v = vb_s[:, 128 * j:128 * (j + 1)]
        return lanes(*[v] * (ch // 128))

    def scaled(n, mlp, get=col):
        return n * get(mlp, 2) + get(mlp, 3)

    def grid_forward():
        p = dot_tn(gw1_ref[...], gx_ref[...].astype(BF)) + col(GRID, 0)
        n, inv = norm_cols(dot_tn(gw2_ref[...], silu_bf(p)) + col(GRID, 1))
        return p, n, inv

    table_s[:, halo:halo + band] = scaled(grid_forward()[1], GRID).astype(BF)
    for c in early:
        c.wait()
    mp = dot_tn(mw1_ref[...], mx_ref[...].astype(BF)) + col(MESH, 0)
    mn, _ = norm_cols(dot_tn(held(15), silu_bf(mp)) + col(MESH, 1))
    hm_s[...] = scaled(mn, MESH).astype(BF)

    pl.semaphore_wait(barrier, len(everyone))
    halos = [copy(table_s.at[:, halo:2 * halo], table_s.at[:, halo + band:nt], hs_sem.at[0], hr_sem.at[0], below),
             copy(table_s.at[:, band:band + halo], table_s.at[:, 0:halo], hs_sem.at[1], hr_sem.at[1], above)]

    hg = table_s[:, halo:halo + band]
    pp = dot_tn(held(5), hg) + col(POST, 0)
    pn, pinv = norm_cols(dot_tn(held(6), silu_bf(pp)) + col(POST, 1))
    grid_out_ref[...] = (hg.astype(F32) + scaled(pn, POST)).T.astype(BF)
    cg = held(7).astype(F32).T
    pd = norm_back(cg * col(POST, 2), pn, pinv)
    pg1 = grad_first(dot_nn(held(6), pd.astype(BF)), pp)
    cotg_s[...] = cg + dot_nn(held(5), pg1)

    wl_s[:, 0:lat] = held(10).T
    wl_s[:, lat:2 * lat] = held(11).T
    ew2t_s[...] = held(14).T
    dw2t_s[...] = dw2_ref[...].T
    pm_s[...] = dot_tn(held(12), hm_s[...]) + col(EDGE, 0)
    agg_s[...] = jnp.zeros_like(agg_s)
    base = me * band - halo

    def slab(i):
        return pl.ds(pl.multiple_of(i * ch, ch), ch)

    def masked_dst(sl):
        return jnp.where(mask_ref[:, sl] > 0, dst_ref[:, sl], -1)

    def embed(i):
        pe = dot_nn(ew1t_s[...], ex_ref[:, slab(i)].astype(BF)) + wcol(EMBED, 0)
        ne, _ = norm_cols(dot_nn(ew2t_s[...], silu_bf(pe)) + wcol(EMBED, 1))
        he_s[slab(i), :] = scaled(ne, EMBED, wcol).astype(BF)

    def first_half(i):
        sl = slab(i)
        gath = dot_nn(table_s[...], one_hot(nt, src_ref[:, sl] - base)).astype(BF)
        pre_s[sl, :] = dot_nn(wl_s[...], rows(he_s[sl, :], gath)) + pick_lanes(pm_s, dst_ref[:, sl])

    def second_half(i):
        sl = slab(i)
        n, inv = norm_cols(dot_nn(dw2t_s[...], silu_bf(pre_s[sl, :])) + wcol(EDGE, 1))
        norm_s[sl, :] = n
        inv_s[i] = inv
        msg = he_s[sl, :].astype(F32) + scaled(n, EDGE, wcol)
        ohm = one_hot(nm, masked_dst(sl))
        agg_s[...] += dot_nt(lanes(*split3(msg)), lanes(ohm, ohm, ohm))

    def fwd(i, carry):
        second_half(i - 1)
        first_half(i)
        embed(jnp.minimum(i + 1, steps - 1))
        return carry

    embed(0)
    embed(1)
    for c in halos:
        c.wait_recv()
    first_half(0)
    lax.fori_loop(1, steps, fwd, 0)
    second_half(steps - 1)

    for c in node:
        c.wait()
    hm = hm_s[...]
    np_ = dot_tn(rows(g1_s[...], g2_s[...]), rows(hm, agg_s[...].astype(BF))) + col(NODE, 0)
    nn_, ninv = norm_cols(dot_tn(act_s[...], silu_bf(np_)) + col(NODE, 1))
    mesh_out_ref[...] = (hm.astype(F32) + scaled(nn_, NODE)).T.astype(BF)
    d2 = norm_back(cotm_ref[...].astype(F32).T * col(NODE, 2), nn_, ninv)
    ng1 = grad_first(dot_nn(act_s[...], d2.astype(BF)), np_)
    ag = dot_nn(g2_s[...], ng1) * col(EDGE, 2)
    pm_s[...] = ag - jnp.mean(ag, axis=0, keepdims=True)

    w1g_s[...] = jnp.zeros_like(w1g_s)
    w2g_s[...] = jnp.zeros_like(w2g_s)

    slots = [(g1_s.at[:, :], g2_s.at[:, :], act_s.at[:, :]),
             (wl_s.at[:, 0:lat], wl_s.at[:, lat:2 * lat], ew2t_s.at[:, :])]

    def second_grad(i, slot):
        sl = slab(i)
        bg = jnp.where(mask_ref[:, sl] > 0, pick_lanes(pm_s, dst_ref[:, sl]), 0.0)
        n = norm_s[sl, :]
        slots[slot][1][...] = (inv_s[i] * (bg - n * jnp.mean(bg * n, axis=0, keepdims=True))).astype(BF)

    def first_grad(i, slot):
        p = pre_s[slab(i), :]
        d_act = dot_nn(dw2_ref[...], slots[slot][1][...])
        slots[slot][2][...] = silu_bf(p)
        slots[slot][0][...] = grad_first(d_act, p)

    def sums(i, slot):
        sl = slab(i)
        g1, g2, act = slots[slot]
        w2g_s[...] += dot_nt(act[...], g2[...])
        w1g_s[...] += dot_nt(rows(he_s[sl, :], one_hot(nt, src_ref[:, sl] - base), one_hot(nm, masked_dst(sl))), g1[...])

    def bwd(j, carry):
        i = 2 * j
        first_grad(i - 1, 1)
        sums(i - 2, 0)
        second_grad(i, 0)
        first_grad(i, 0)
        sums(i - 1, 1)
        second_grad(i + 1, 1)
        return carry

    second_grad(0, 0)
    first_grad(0, 0)
    second_grad(1, 1)
    lax.fori_loop(1, steps // 2, bwd, 0)
    for peer in everyone:
        pl.semaphore_signal(done_sem, inc=1, device_id=peer, device_id_type=DEV)
    first_grad(steps - 1, 1)
    sums(steps - 2, 0)
    sums(steps - 1, 1)

    half = lat // 2
    q = half // 2
    mine = pl.multiple_of(core * half, half)
    his = pl.multiple_of((1 - core) * half, half)
    his_b = pl.multiple_of(his + q, q)
    n1, n2 = 3 * lat, lat

    def swap(k, src, top, c0, w, j):
        return copy(src, pre_s.at[top:top + src.shape[0], c0:c0 + w], send0.at[j], recv0.at[j], partner)

    pl.semaphore_wait(done_sem, len(everyone))
    late = [fetch(3, dw1_ref.at[lat:2 * lat, :], 8)]
    first = {'c': [swap('c', w2g_s.at[:, pl.ds(his, half)], n1, 0, half, 0)],
             'a': [swap('a', w1g_s.at[0:lat, pl.ds(his, q)], 0, 0, q, 1)],
             'b': [swap('b', w1g_s.at[0:lat, pl.ds(his_b, q)], 0, q, q, 2)]}
    for k, part in enumerate(split3(w1g_s[lat:lat + nt, :])):
        he_s[k * nt:(k + 1) * nt, :] = part
    t0 = 9 * lat
    for k, part in enumerate(split3(w1g_s[lat + nt:lat + nt + nm, :])):
        he_s[t0 + k * nm:t0 + (k + 1) * nm, :] = part
    tb = table_s[...]
    w1g_s[lat:2 * lat, :] = dot_nn(lanes(tb, tb, tb), he_s[0:3 * nt, :])
    w1g_s[2 * lat:3 * lat, :] = dot_nn(lanes(hm, hm, hm), he_s[t0:t0 + 3 * nm, :])
    first['a'].append(swap('a', w1g_s.at[lat:n1, pl.ds(his, q)], lat, 0, q, 3))
    first['b'].append(swap('b', w1g_s.at[lat:n1, pl.ds(his_b, q)], lat, q, q, 4))

    b1, b2 = n1 // 64, n2 // 64
    shape = {'a': (b1, 0, q), 'b': (b1, q, q), 'c': (b2, 0, half)}
    axes = {'a': 'xyz', 'b': 'yzx', 'c': 'zxy'}
    order = 'cab'
    at = {'a': 0, 'b': 0, 'c': n1}
    acc_rows = {k: [] for k in order}
    buf_rows = {k: [] for k in order}
    top_a, top_b = 4 * lat, n1 + n2
    for stage in range(4):
        for k in 'ac':
            acc_rows[k].append(top_a)
            top_a += shape[k][0] * 4 ** (3 - stage)
            buf_rows[k].append(top_b)
            top_b += 0 if stage == 3 else 3 * shape[k][0] * 4 ** (2 - stage)
    acc_rows['b'], buf_rows['b'] = acc_rows['a'], buf_rows['a']

    def acc_at(k, stage, off, n):
        return norm_s.at[pl.ds(acc_rows[k][stage] + off, n), shape[k][1]:shape[k][1] + shape[k][2]]

    def buf_at(k, stage, off, n):
        return pre_s.at[pl.ds(buf_rows[k][stage] + off, n), shape[k][1]:shape[k][1] + shape[k][2]]

    def send(k, stage, j, src_off, dst_off, n, d):
        c = copy(acc_at(k, stage, src_off, n), buf_at(k, stage, dst_off, n), sends.at[order.index(k), stage, j],
                 recvs.at[order.index(k), stage, j], peers[axes[k][stage]][d - 1])
        started.append(c)
        return c

    def block(k, stage, d, n, off=0):
        return pl.multiple_of(turn(pos[axes[k][stage]], d) * n + off, 8)

    def launch(k, stage):
        n = shape[k][0] * 4 ** (2 - stage)
        return [send(k, stage, d - 1, block(k, stage, d, n), (d - 1) * n, n, d) for d in (2, 1, 3)]

    started = list(halos)
    flying = {}

    def open_first(k):
        n, c0, w = shape[k]
        for c in first[k]:
            c.wait_recv()
            started.append(c)
        src = w2g_s if k == 'c' else w1g_s
        for i in range(64):
            v = {'z': i // 16, 'y': i // 4 % 4, 'x': i % 4}
            to = (v[axes[k][0]] * 4 + v[axes[k][1]]) * 4 + v[axes[k][2]]
            acc_at(k, 0, to * n, n)[...] = (src[i * n:(i + 1) * n, pl.ds(pl.multiple_of(mine + c0, q), w)]
                                            + pre_s[at[k] + i * n:at[k] + (i + 1) * n, c0:c0 + w])
        n = n * 16
        h = n // 2
        flying[k] = [send(k, 0, 0, block(k, 0, 2, n), 0, h, 1), send(k, 0, 1, block(k, 0, 2, n, h), h, h, 3),
                     send(k, 0, 2, block(k, 0, 1, n, h), n + h, h, 1), send(k, 0, 3, block(k, 0, 3, n), 2 * n, h, 3)]

    def relay_first(k):
        n = shape[k][0] * 16
        h = n // 2
        for j, d, off, dst in ((0, 1, 0, n), (1, 3, h, 2 * n + h)):
            flying[k][j].wait_recv()
            to = acc_at(k, 0, block(k, 0, d, n, off), h)
            to[...] = to[...] + buf_at(k, 0, j * h, h)[...]
            flying[k].append(send(k, 0, 4 + j, block(k, 0, d, n, off), dst, h, d))

    def close_first(k):
        n = shape[k][0] * 16
        for c in flying[k][2:]:
            c.wait_recv()
        acc_at(k, 1, 0, n)[...] = acc_at(k, 0, block(k, 0, 0, n), n)[...] + (
            buf_at(k, 0, n, n)[...] + buf_at(k, 0, 2 * n, n)[...])
        flying[k] = launch(k, 1)

    open_first('c')
    for c in late:
        c.wait()
    wb = held(8)
    tg = dot_nt(lanes(wb, wb, wb), lanes(he_s[0:nt, :], he_s[nt:2 * nt, :], he_s[2 * nt:3 * nt, :]))
    norm_s[0:lat, 0:halo] = tg[:, 0:halo]
    norm_s[0:lat, halo:2 * halo] = tg[:, halo + band:nt]
    norm_s[lat:2 * lat, :] = tg[:, halo:halo + band]
    tails = [copy(norm_s.at[0:lat, 0:halo], pre_s.at[0:lat, 2 * halo:3 * halo], ts_sem.at[0], tr_sem.at[0], below),
             copy(norm_s.at[0:lat, halo:2 * halo], pre_s.at[0:lat, 3 * halo:4 * halo], ts_sem.at[1], tr_sem.at[1],
                  above)]
    started += tails
    open_first('a')
    open_first('b')

    gp, gn, ginv = grid_forward()
    keep_p, keep_n = slice(10 * lat, 11 * lat), slice(11 * lat, 12 * lat)
    norm_s[keep_p, :] = gp
    norm_s[keep_n, :] = gn
    inv_s[0] = ginv
    relay_first('c')
    relay_first('a')
    relay_first('b')
    own = cotg_s[...] + norm_s[lat:2 * lat, :]

    for c in tails:
        c.wait_recv()
    ends = lanes(own[:, 0:halo] + pre_s[0:lat, 3 * halo:4 * halo], own[:, halo:band - halo],
                 own[:, band - halo:band] + pre_s[0:lat, 2 * halo:3 * halo])
    gd = norm_back(ends * col(GRID, 2), norm_s[keep_n, :], inv_s[0])
    close_first('c')
    gg1 = grad_first(dot_nn(gw2_ref[...], gd.astype(BF)), norm_s[keep_p, :])
    ggrad_ref[...] = dot_nn(gw1_ref[...], gg1)
    close_first('a')
    close_first('b')

    for stage in (1, 2):
        for k in order:
            for c in flying[k]:
                c.wait_recv()
            n = shape[k][0] * 4 ** (2 - stage)
            acc_at(k, stage + 1, 0, n)[...] = (
                acc_at(k, stage, block(k, stage, 0, n), n)[...] + buf_at(k, stage, 0, n)[...]) + (
                buf_at(k, stage, n, n)[...] + buf_at(k, stage, 2 * n, n)[...])
            if stage < 2:
                flying[k] = launch(k, stage + 1)

    r1, r2 = o1_ref.shape[0], o2_ref.shape[0]
    win = r1 + r2
    f1, f2 = acc_rows['a'][3], acc_rows['c'][3]
    e1, e2 = top_b, top_b + win
    last = [copy(norm_s.at[pl.ds(pl.multiple_of(f1 + (1 - core) * 8, 8), win), 0:half], pre_s.at[e1:e1 + win, 0:half],
                 send4.at[0], recv4.at[0], partner),
            copy(norm_s.at[f2:f2 + b2, 0:half], pre_s.at[e2:e2 + b2, 0:half], send4.at[1], recv4.at[1], partner)]
    own1 = norm_s[pl.ds(pl.multiple_of(f1 + core * 8, 8), win), 0:half]
    own2 = norm_s[f2:f2 + b2, 0:half]
    low = core == 0
    o1_ref[:, pl.ds(mine, half)] = jnp.where(low, own1[0:r1], own1[r2:win])
    o2_ref[:, pl.ds(mine, half)] = jnp.where(low, own2[0:r2], own2[r2:b2])
    for c in last:
        c.wait_recv()
    got1 = pre_s[e1:e1 + win, 0:half]
    got2 = pre_s[e2:e2 + b2, 0:half]
    o1_ref[:, pl.ds(his, half)] = jnp.where(low, got1[0:r1], got1[r2:win])
    o2_ref[:, pl.ds(his, half)] = jnp.where(low, got2[0:r2], got2[r2:b2])
    for c in started + last:
        c.wait_send()


def finish_kernel(*refs):
    n = (len(refs) - 1) // 3
    bufs, sems = refs[2 * n:3 * n], refs[3 * n]
    ins = [pltpu.make_async_copy(refs[k], bufs[k], sems.at[0, k]) for k in range(n)]
    outs = [pltpu.make_async_copy(bufs[k], refs[n + k], sems.at[1, k]) for k in range(n)]
    for c in ins:
        c.start()
    for c, o in zip(ins, outs):
        c.wait()
        o.start()
    for o in outs:
        o.wait()


def finish_call(outs):
    n = len(outs)
    return pl.pallas_call(
        finish_kernel,
        out_shape=tuple(jax.ShapeDtypeStruct(o.shape, o.dtype) for o in outs),
        in_specs=[pl.BlockSpec(memory_space=pl.ANY)] * n,
        out_specs=(pl.BlockSpec(memory_space=pl.ANY),) * n,
        scratch_shapes=[VMEM(o.shape, o.dtype) for o in outs] + [pltpu.SemaphoreType.DMA((2, n))],
        compiler_params=pltpu.CompilerParams(vmem_limit_bytes=67043328),
        name='finish',
    )(*outs)


def step_call(args, sizes):
    band, nm, edges, lat, feats = sizes
    steps = edges // CHUNK
    nt = band + band // 2
    dma = pltpu.SemaphoreType.DMA
    out_shape = (jax.ShapeDtypeStruct((nm, lat), BF), jax.ShapeDtypeStruct((band, lat), BF),
                 jax.ShapeDtypeStruct((feats, band), F32), jax.ShapeDtypeStruct((3 * lat // 128, lat), F32),
                 jax.ShapeDtypeStruct((lat // 128, lat), F32))
    return pl.pallas_call(
        step_kernel,
        out_shape=out_shape,
        in_specs=[pl.BlockSpec(memory_space=pl.ANY if k in FETCHED else VMEM) for k in range(len(args))],
        out_specs=(pl.BlockSpec(memory_space=VMEM),) * len(out_shape),
        scratch_shapes=[VMEM((edges, CHUNK), F32), VMEM((edges, CHUNK), F32), VMEM((steps * lat, CHUNK), BF),
                        VMEM((steps, 1, CHUNK), F32), VMEM((lat, 2 * lat), BF), VMEM((lat, nm), F32),
                        VMEM((lat, nm), F32), VMEM((lat, CHUNK), BF), VMEM((lat, CHUNK), BF), VMEM((lat, CHUNK), BF),
                        VMEM((lat, band), F32),
                        VMEM((3 * lat, lat), F32), VMEM((lat, lat), F32), VMEM((lat, nt), BF),
                        VMEM((lat, nm), BF), VMEM((lat, lat), BF), VMEM((lat, lat), BF),
                        VMEM((lat, 128), F32), VMEM((lat, 7 * 128), F32), VMEM((lat, 4), BF),
                        dma((10,)), pltpu.SemaphoreType.REGULAR, dma((2,)), dma((2,)), dma((2,)), dma((2,)),
                        dma((5,)), dma((5,)), dma((3, 3, 6)), dma((3, 3, 6)), dma((2,)), dma((2,))],
        compiler_params=pltpu.CompilerParams(collective_id=0, has_side_effects=True, vmem_limit_bytes=67043328),
        name='whole_step',
    )(*args)


def solution(mesh):
    row_spec = P(('batch', 'graph'), None)
    flat_spec = P(('batch', 'graph'))
    rep_spec = P(None, None)

    def device_step(grid_in, mesh_in, edge_in, edge_src, edge_dst, edge_mask, *rest):
        sizes = (grid_in.shape[0], mesh_in.shape[0], edge_in.shape[0], rest[1].shape[1], grid_in.shape[1])
        args = (grid_in.T, mesh_in.T, edge_in.T, edge_src[None], edge_dst[None], edge_mask[None]) + rest
        mesh_out, grid_out, ggrad, w1_grad, w2_grad = finish_call(step_call(args, sizes))
        return mesh_out, grid_out, ggrad.T, w1_grad, w2_grad

    in_specs = (row_spec, row_spec, row_spec, flat_spec, flat_spec, flat_spec) + (rep_spec,) * 18 + (row_spec, row_spec)
    return jax.shard_map(device_step, mesh=mesh, in_specs=in_specs, out_specs=(row_spec,) * 5, check_vma=False)
```

profile of v0, /device:TPU:1, one launch (start us, length us, event | category | flops | bytes accessed | tf_op | source)
XLA Modules:
  0.0 130.7 jit_solution(16172996961033463630)
XLA Ops:
  0.6 127.8 %whole_step.1 = (bf16[256,512]{1,0:T(8,128)(2,1)}, bf16[512,512]{1,0:T(8,128)(2,1)}, f32[186,512]{1,0:T(8,128)}, f32[12,512]{1,0:T(8,128)}, f32[4,512]{1,0:T(4,128)}) custom-call(f32[186,512]{1,0:T(8,128)} %bitcast.7, f32[3,256]{1,0:T(4,128)} %bitcast.12, f32[4,8192]{1,0:T(4,128)} %bitcast.8, s32[1,8192]{1,0:T(1,128)} %bitcast.9, s32[1,8192]{1,0:T(1,128)} %bitcast.10, ...), custom_call_target="tpu_custom_call" | custom-call | tf_op jit(solution)/shard_map/whole_step/pallas_call | solution.py:498
  128.4 2.1 %finish.1 = (bf16[256,512]{1,0:T(8,128)(2,1)}, bf16[512,512]{1,0:T(8,128)(2,1)}, f32[186,512]{1,0:T(8,128)}, f32[12,512]{1,0:T(8,128)}, f32[4,512]{1,0:T(4,128)}) custom-call(bf16[256,512]{1,0:T(8,128)(2,1)} %get-tuple-element.15.refs_0_, bf16[512,512]{1,0:T(8,128)(2,1)} %get-tuple-element.16.refs_1_, f32[186,512]{1,0:T(8,128)} %get-tuple-element.17.refs_2_, ...), custom_call_target="tpu_custom_call" | custom-call | tf_op jit(solution)/shard_map/finish/pallas_call | solution.py:479
where the time goes:
time: 131 us
  Pallas kernels  130 us (99%)
    pallas_call x1, Pallas kernels, step_call(): pl.pallas_call(step_kernel, out_shape=out_shape, in_specs=[pl.BlockSpec(m...  128 us

commit v1 on v0

--- a/solution.py
+++ b/solution.py
@@ -227,8 +227,8 @@
 
     def fwd(i, carry):
         second_half(i - 1)
+        embed(jnp.minimum(i + 1, steps - 1))
         first_half(i)
-        embed(jnp.minimum(i + 1, steps - 1))
         return carry
 
     embed(0)

time: 131 us -> 132 us (level)
  no operation moved by 1% of the time
where the time goes in v1:
time: 132 us
  Pallas kernels  131 us (99%)
    pallas_call x1, Pallas kernels, step_call(): pl.pallas_call(step_kernel, out_shape=out_shape, in_specs=[pl.BlockSpec(m...  129 us

profile of v1, /device:TPU:1, one launch (start us, length us, event | category | flops | bytes accessed | tf_op | source)
XLA Modules:
  0.0 131.6 jit_solution(9926667890422856351)
XLA Ops:
  0.6 128.6 %whole_step.1 = (bf16[256,512]{1,0:T(8,128)(2,1)}, bf16[512,512]{1,0:T(8,128)(2,1)}, f32[186,512]{1,0:T(8,128)}, f32[12,512]{1,0:T(8,128)}, f32[4,512]{1,0:T(4,128)}) custom-call(f32[186,512]{1,0:T(8,128)} %bitcast.7, f32[3,256]{1,0:T(4,128)} %bitcast.12, f32[4,8192]{1,0:T(4,128)} %bitcast.8, s32[1,8192]{1,0:T(1,128)} %bitcast.9, s32[1,8192]{1,0:T(1,128)} %bitcast.10, ...), custom_call_target="tpu_custom_call" | custom-call | tf_op jit(solution)/shard_map/whole_step/pallas_call | solution.py:498
  129.3 2.1 %finish.1 = (bf16[256,512]{1,0:T(8,128)(2,1)}, bf16[512,512]{1,0:T(8,128)(2,1)}, f32[186,512]{1,0:T(8,128)}, f32[12,512]{1,0:T(8,128)}, f32[4,512]{1,0:T(4,128)}) custom-call(bf16[256,512]{1,0:T(8,128)(2,1)} %get-tuple-element.15.refs_0_, bf16[512,512]{1,0:T(8,128)(2,1)} %get-tuple-element.16.refs_1_, f32[186,512]{1,0:T(8,128)} %get-tuple-element.17.refs_2_, ...), custom_call_target="tpu_custom_call" | custom-call | tf_op jit(solution)/shard_map/finish/pallas_call | solution.py:479
